TPU v7x, 32 devices: a whole 2x2x4 slice. The times are simulated.
32 devices in a mesh: dp: 4 (over x, y), tp: 8 (over z, core).
Axes of the slice: x: 2, y: 2, z: 4, core: 2. Of those that a mesh axis runs over, the one named last changes fastest.
Arguments:
- hidden: bfloat16 [4, 3072, 3072], P('dp', 'tp'), parts along dimension 0
- targets: int32 [4, 3072], P('dp', 'tp'), parts along dimension 0
- norm_gain: bfloat16 [3072], replicated
- head_w: bfloat16 [128256, 3072], P('tp')
- temperature: float32 [], replicated
Outputs:
- output 1: float32 [4, 3072], P('dp', 'tp'), parts along dimension 0
- output 2: float32 [4, 3072], P('dp', 'tp'), parts along dimension 0
There are 4 independent parts. A program takes and returns all parts, laid end to end along the dimension named above; an argument that names none is the same for every part.
All inputs are finite; a program needn't handle non-finite values.
Results may differ from a plain program's by a relative error of at most 0.001.
Values are sent between devices in bfloat16 or wider.
A program may use at most 1 GiB of HBM per device.

v0:
```python
import jax
import jax.numpy as jnp
from jax import lax
from jax.sharding import PartitionSpec as P

NORM_EPS = 1e-6


def solution(mesh):
    def device_body(h_loc, target_loc, norm_gain, w_loc, value_a11):
        tok_loc = h_loc.shape[1]
        vocab_loc = w_loc.shape[0]
        shard_idx = lax.axis_index('tp')
        h_wide = h_loc.astype(jnp.float32)
        inv_rms = lax.rsqrt(jnp.mean(h_wide * h_wide, axis=-1, keepdims=True) + NORM_EPS)
        normed = (norm_gain.astype(jnp.float32) * h_wide * inv_rms).astype(jnp.bfloat16)
        normed_all = lax.all_gather(normed, 'tp', axis=1, tiled=True)
        target_all = lax.all_gather(target_loc, 'tp', axis=1, tiled=True)
        logits = jnp.einsum('rsd,vd->rsv', normed_all, w_loc, preferred_element_type=jnp.float32) / value_a11
        local_max = jnp.max(logits, axis=-1)
        top_val = lax.pmax(local_max, 'tp')
        exp_shift = jnp.exp(logits - top_val[..., None])
        sum_exp = jnp.sum(exp_shift, axis=-1)
        weighted = jnp.sum(exp_shift * logits, axis=-1)
        vocab_ids = lax.broadcasted_iota(jnp.int32, (1, 1, vocab_loc), 2) + shard_idx * vocab_loc
        target_logit = jnp.sum(jnp.where(vocab_ids == target_all[..., None], logits, 0.0), axis=-1)
        stacked = jnp.stack([sum_exp, weighted, target_logit])
        own_sums = lax.psum_scatter(stacked, 'tp', scatter_dimension=2, tiled=True)
        own_max = lax.dynamic_slice_in_dim(top_val, shard_idx * tok_loc, tok_loc, axis=1)
        log_norm = own_max + jnp.log(own_sums[0])
        return own_sums[2] - log_norm, log_norm - own_sums[1] / own_sums[0]

    return jax.shard_map(
        device_body,
        mesh=mesh,
        in_specs=(P('dp', 'tp', None), P('dp', 'tp'), P(), P('tp', None), P()),
        out_specs=(P('dp', 'tp'), P('dp', 'tp')),
        check_vma=False,
    )
```

profile of v0, /device:TPU:0, one launch (start us, length us, event | category | flops | bytes accessed | tf_op | source)
XLA Modules:
  0.0 662.1 jit_solution(6136546780165897126)
XLA Ops:
  7.2 0.0 all-gather.2.cloned.1.call-start
  7.2 0.7 convert_element_type.9
  7.9 2.2 fusion.4
  10.1 3.8 fusion.3
  14.0 0.0 all-gather.2.cloned.1.call-update
  14.0 0.0 reduce-scatter.4.cloned.1.call-start
  14.7 15.6 %all_gather.7 = s32[1,3072]{1,0:T(1,128)} all-gather(s32[1,384]{1,0:T(1,128)} %param.6), channel_id=1, replica_groups=mesh['dp'=4,'tp'=8] {'tp'}, dimensions={1}, use_global_device_ids=true | all-gather | bytes 13824 | tf_op jit(solution)/shard_map/all_gather | solution.py:18
  30.3 0.6 iota_add_fusion
  30.9 154.3 %all-gather.2.cloned.1.call-done = bf16[1,3072,3072]{2,1,0:T(8,128)(2,1)} async-done(((bf16[1,384,3072]{2,1,0:T(8,128)(2,1)}), bf16[1,3072,3072]{2,1,0:T(8,128)(2,1)}) %all-gather.2.cloned.1.call-update) | async-done | bytes 18874384 | tf_op jit(solution)/shard_map/all_gather | solution.py:17
  185.2 0.0 copy-start
  185.2 0.0 copy-start.1
  185.2 320.8 %fusion.6 = (f32[3072]{0:T(1024)S(1)}, f32[3072,16032]{0,1:T(8,128)}) fusion(f32[]{:T(128)S(6)} %copy.12, bf16[16032,3072]{1,0:T(8,128)(2,1)} %param.8, bf16[1,3072,3072]{2,1,0:T(8,128)(2,1)} %all-gather.2.cloned.1.call-done), kind=kOutput, calls=%fused_computation.20 | convolution fusion | flops 302692368384 | bytes 314388480 | tf_op jit(solution)/shard_map/rsd,vd->rsv/dot_general | solution.py:19
  506.0 26.7 %pmax.7 = f32[1,3072]{1,0:T(1,128)S(1)} all-reduce(f32[1,3072]{1,0:T(1,128)S(1)} %bitcast.31), channel_id=1, replica_groups=mesh['dp'=4,'tp'=8] {'tp'}, use_global_device_ids=true, to_apply=%region_2.0 | all-reduce | flops 3072 | bytes 24576 | tf_op jit(solution)/shard_map/pmax | solution.py:21
  532.7 0.0 copy-done
  532.7 0.0 copy-done.1
  532.7 74.8 %fusion = (f32[3072]{0:T(1024)S(1)}, f32[3072]{0:T(1024)S(1)}, f32[3072]{0:T(1024)S(1)}) fusion(f32[3072,16032]{0,1:T(8,128)} %get-tuple-element.11, f32[3072]{0:T(1024)S(1)} %bitcast.26, s32[3072]{0:T(1024)S(1)} %bitcast.30, s32[16032]{0:T(1024)S(1)} %copy-done), kind=kLoop, calls=%fused_computation.3 | loop fusion | flops 344742912 | bytes 197126784 | tf_op jit(solution)/shard_map/reduce_sum | solution.py:23
  607.6 4.5 copy.7
  612.1 7.9 %bitcast_reduce_fusion = f32[3072,3]{1,0:T(8,128)} fusion(f32[3,1,3072]{1,0,2:T(4,128)} %copy.7), kind=kLoop, calls=%fused_computation.6 | loop fusion | bytes 73728
  620.0 0.0 reduce-scatter.4.cloned.1.call-update
  620.0 32.5 %reduce-scatter.4.cloned.1.call-done = f32[384,3]{1,0:T(8,128)} async-done(((f32[3072,3]{1,0:T(8,128)}), f32[384,3]{1,0:T(8,128)}) %reduce-scatter.4.cloned.1.call-update) | async-done | bytes 4624
  652.6 1.4 reshape_bitcast_fusion
  654.0 0.4 fusion.5
  654.4 0.1 copy.10
  654.5 0.1 copy.11
  654.6 0.1 copy.9
  654.7 0.6 bitcast_subtract_fusion
  (2 shorter events, 0.0 us)
Async XLA Ops:
  7.2 178.1 %all-gather.2.cloned.1.call-start = ((), (), s32[]{:S(2)}) async-start(), calls=%async_computation.1 | async-start | bytes 21233664 | tf_op jit(solution)/shard_map/all_gather | solution.py:17
  14.0 638.6 %reduce-scatter.4.cloned.1.call-start = ((), (), s32[]{:S(2)}) async-start(), calls=%async_computation.2 | async-start | bytes 1769472
  185.2 347.5 %copy-start = (s32[16032]{0:T(1024)S(1)}, s32[16032]{0:T(1024)}, u32[]{:S(2)}) copy-start(s32[16032]{0:T(1024)} %iota_add_fusion) | copy-start | bytes 192388
  185.2 347.5 %copy-start.1 = (s32[1,3072]{1,0:T(1,128)S(1)}, s32[1,3072]{1,0:T(1,128)}, u32[]{:S(2)}) copy-start(s32[1,3072]{1,0:T(1,128)} %all_gather.7) | copy-start | bytes 36868
Sparse Core Ops, SparseCore 0:
  14.1 171.0 all-gather.1
  620.1 32.3 reduce-scatter.3
where the time goes:
time: 662 us
  matrix products  321 us (48%)
  waiting for transfers between devices  187 us (28%)
  other arithmetic  82.8 us (13%)
  blocking collectives  42.3 us (6%)
  between operations  14.7 us (2%)
  local copies, waits for them, and re-layouts  14.5 us (2%)
    dot_general x1, matrix products, device_body(): jnp.einsum('rsd,vd->rsv', normed_all, w_loc, preferred_element_type=jnp.f...  321 us
    all_gather x1, waiting for transfers between devices, device_body(): normed_all = lax.all_gather(normed, 'tp', axis=1, tiled=True)  154 us
    reduce_sum x1, other arithmetic, device_body(): sum_exp = jnp.sum(exp_shift, axis=-1)  74.8 us
    unnamed x3, waiting for transfers between devices  32.6 us
    pmax x1, blocking collectives, device_body(): top_val = lax.pmax(local_max, 'tp')  26.7 us
    all_gather x1, blocking collectives, device_body(): target_all = lax.all_gather(target_loc, 'tp', axis=1, tiled=True)  15.6 us
    unnamed x10, local copies, waits for them, and re-layouts  14.1 us
  transfers between devices with their start and end apart: 2, of which 2 were waited for; matrix products, arithmetic and copies ran while one was open for 0% of the time, Pallas kernels for 0%

commit v1 on v0

v1 whole, which is shorter than its diff:
```python
import functools

import jax
import jax.numpy as jnp
from jax import lax
from jax.experimental import pallas as pl
from jax.experimental.pallas import tpu as pltpu
from jax.sharding import PartitionSpec as P

NORM_EPS = 1e-6
F32 = jnp.float32
LANES = 128
SPLITS = (672, 672, 672, 656)
GROUP = 64
CHIPS = 4
CORES = 2
PEERS = CHIPS * CORES
FORWARD_TRIPS = (5, 10, 15)
MESH = pl.DeviceIdType.MESH


def _tree(op, values):
    while len(values) > 1:
        paired = [op(a, b) for a, b in zip(values[::2], values[1::2])]
        values = paired + values[len(values) & ~1:]
    return values[0]


def _xor(a, b):
    return (a % 2 + b % 2) % 2 + 2 * ((a // 2 + b // 2) % 2)


def _online(z_ref, rows, inv_tau, first_id, target, stats, cols, width):
    m_ref, s_ref, w_ref, t_ref = stats
    m, s, w, t = m_ref[:, cols], s_ref[:, cols], w_ref[:, cols], t_ref[:, cols]
    rel = target - first_id - lax.broadcasted_iota(jnp.int32, (8, width), 0)
    for r0 in range(0, rows, GROUP):
        n = min(GROUP, rows - r0)
        block = z_ref[r0:r0 + n, :] * inv_tau
        z = [block[i:i + 8] for i in range(0, n, 8)]
        m_new = jnp.maximum(m, _tree(jnp.maximum, z))
        keep = jnp.exp(m - m_new)
        p = [jnp.exp(v - m_new) for v in z]
        s = s * keep + _tree(jnp.add, p)
        w = w * keep + _tree(jnp.add, [a * b for a, b in zip(p, z)])
        for i, v in enumerate(z):
            t = jnp.where(rel == r0 + 8 * i, v, t)
        m = m_new
    m_ref[:, cols], s_ref[:, cols], w_ref[:, cols], t_ref[:, cols] = m, s, w, t


def _kernel(tok, vocab, depth, tau_ref, h_hbm, tgt_hbm, gain_ref, w_hbm, logp_ref, ent_ref,
            xs, wbuf, z0, z1, z2, z3, tgt_all, m_ref, s_ref, w_ref, t_ref, part, landed,
            h_sem, t_sem, w_sem, own_send, own_recv, recv, send_p, send_r, send_l, tgt_send, tgt_recv, st_send, st_recv):
    zs = (z0, z1, z2, z3)
    stats = (m_ref, s_ref, w_ref, t_ref)
    me = lax.axis_index('tp')
    chip, core = me // CORES, me % CORES
    other = me + 1 - 2 * core
    right, left = (me + CORES) % PEERS, (me + PEERS - CORES) % PEERS
    rows = sum(SPLITS)
    chunks = vocab // rows
    width = CORES * tok
    tiles = tok // LANES
    trips = CHIPS * chunks
    offs = [sum(SPLITS[:i]) for i in range(len(SPLITS))]
    last = len(SPLITS) - 1

    def load_h(i):
        r = pl.ds(i * LANES, LANES)
        return pltpu.make_async_copy(h_hbm.at[r], wbuf.at[1, r], h_sem.at[i])

    def load_w(t, slot):
        r = pl.ds(pl.multiple_of((t % chunks) * rows, 16), rows)
        return pltpu.make_async_copy(w_hbm.at[r], wbuf.at[slot], w_sem.at[slot])

    def block_at(b):
        return xs.at[pl.ds(b * tiles, tiles)]

    def hop(b, dst, sems):
        return pltpu.make_async_remote_copy(
            src_ref=block_at(b), dst_ref=block_at(b), send_sem=sems.at[b], recv_sem=recv.at[b],
            device_id={'tp': dst}, device_id_type=MESH)

    def own_piece(i, b):
        piece = xs.at[b * tiles + i]
        return pltpu.make_async_remote_copy(
            src_ref=piece, dst_ref=piece, send_sem=own_send.at[i], recv_sem=own_recv.at[i],
            device_id={'tp': other}, device_id_type=MESH)

    def tgt_cols(b):
        return pl.ds(pl.multiple_of(b * tok, LANES), tok)

    def send_tgt(d, b):
        c = tgt_all.at[:, tgt_cols(b)]
        return pltpu.make_async_remote_copy(
            src_ref=c, dst_ref=c, send_sem=tgt_send.at[d], recv_sem=tgt_recv.at[d],
            device_id={'tp': (me + d) % PEERS}, device_id_type=MESH)

    def send_stat(d, src, slot):
        return pltpu.make_async_remote_copy(
            src_ref=part.at[src], dst_ref=landed.at[slot], send_sem=st_send.at[d], recv_sem=st_recv.at[d],
            device_id={'tp': (me + d) % PEERS}, device_id_type=MESH)

    for i in range(tiles):
        load_h(i).start()
    own_tgt = pltpu.make_async_copy(tgt_hbm, tgt_all.at[:, tgt_cols(me)], t_sem)
    own_tgt.start()
    load_w(0, 0).start()
    barrier = pltpu.get_barrier_semaphore()
    for d in range(1, PEERS):
        pl.semaphore_signal(barrier, inc=1, device_id={'tp': (me + d) % PEERS}, device_id_type=MESH)

    inv_tau = 1.0 / tau_ref[0]
    m_ref[...] = jnp.full(m_ref.shape, -jnp.inf, F32)
    for ref in (s_ref, w_ref, t_ref):
        ref[...] = jnp.zeros(ref.shape, F32)
    spare = pl.ds(CHIPS * width, width)
    tgt_all[:, spare] = jnp.full((1, width), -1, jnp.int32)
    z3[...] = jnp.zeros(z3.shape, F32)

    def normalise(i):
        load_h(i).wait()
        r = pl.ds(i * LANES, LANES)
        acc = jnp.zeros((LANES, LANES), F32)
        for k in range(depth // LANES):
            v = wbuf[1, r, k * LANES:(k + 1) * LANES].astype(F32)
            acc = acc + v * v
        inv_rms = lax.rsqrt(jnp.sum(acc, axis=-1, keepdims=True) / depth + NORM_EPS)
        for k in range(depth // LANES):
            c = slice(k * LANES, (k + 1) * LANES)
            v = gain_ref[:, c].astype(F32) * wbuf[1, r, c].astype(F32) * inv_rms
            xs[me * tiles + i, c, :] = v.astype(jnp.bfloat16).T

    normalise(0)
    pl.semaphore_wait(barrier, PEERS - 1)
    own_tgt.wait()
    for d in range(1, PEERS):
        send_tgt(d, me).start()
    for i in range(1, tiles):
        normalise(i)
        own_piece(i - 1, me).start()
    own_piece(tiles - 1, me).start()

    @pl.when(chip < CHIPS - 1)
    def _():
        hop(me, right, send_r).start()

    @pl.when(chip > 0)
    def _():
        hop(me, left, send_l).start()

    for d in range(1, PEERS):
        send_tgt(d, (me + PEERS - d) % PEERS).wait_recv()
    for i in range(tiles):
        own_piece(i, other).wait_recv()

    def pass_on(k):
        @pl.when(chip >= k)
        def _():
            b = (me + PEERS - CORES * k) % PEERS
            hop(b, right, send_r).wait_recv()
            hop(b, other, send_p).start()

            @pl.when(chip < CHIPS - 1)
            def _():
                hop(b, right, send_r).start()

        @pl.when(chip + k < CHIPS)
        def _():
            b = (me + CORES * k) % PEERS
            hop(b, left, send_l).wait_recv()
            hop(b, other, send_p).start()

            @pl.when(chip > 0)
            def _():
                hop(b, left, send_l).start()

    def take_partners(k):
        @pl.when(chip >= k)
        def _():
            hop((other + PEERS - CORES * k) % PEERS, other, send_p).wait_recv()

        @pl.when(chip + k < CHIPS)
        def _():
            hop((other + CORES * k) % PEERS, other, send_p).wait_recv()

    def dot(slot, at, i):
        x = jnp.concatenate([xs[at * CORES * tiles + j] for j in range(CORES * tiles)], axis=1)
        zs[i][...] = jnp.dot(wbuf[slot, offs[i]:offs[i] + SPLITS[i], :], x, preferred_element_type=F32)

    def fold(c, at, i):
        cols = pl.ds(pl.multiple_of(at * width, LANES), width)
        _online(zs[i], SPLITS[i], inv_tau, me * vocab + c * rows + offs[i], tgt_all[:, cols], stats, cols, width)

    def trip(t, carry):
        slot = t % 2
        p, c = t // chunks, t % chunks
        before = jnp.maximum(t - 1, 0)
        at = _xor(chip, p)
        at_before = jnp.where(t == 0, CHIPS, _xor(chip, before // chunks))
        for k in range(1, CHIPS):
            @pl.when(t == FORWARD_TRIPS[k - 1])
            def _(k=k):
                pass_on(k)

            @pl.when(t == k * chunks)
            def _(k=k):
                take_partners(k)
        load_w(t, slot).wait()

        @pl.when(t + 1 < trips)
        def _():
            load_w(t + 1, 1 - slot).start()

        for i in range(len(SPLITS)):
            dot(slot, at, i)
            if i:
                fold(c, at, i - 1)
            else:
                fold(before % chunks, at_before, last)
        return carry

    lax.fori_loop(0, trips, trip, 0)
    fold(chunks - 1, _xor(chip, CHIPS - 1), last)

    for b in range(PEERS):
        cols = slice(b * tok, (b + 1) * tok)
        m8 = m_ref[:, cols]
        m = jnp.max(m8, axis=0, keepdims=True)
        keep = jnp.exp(m8 - m)
        part[b, 0:1, :] = m
        part[b, 1:2, :] = jnp.sum(s_ref[:, cols] * keep, axis=0, keepdims=True)
        part[b, 2:3, :] = jnp.sum(w_ref[:, cols] * keep, axis=0, keepdims=True)
        part[b, 3:4, :] = jnp.sum(t_ref[:, cols], axis=0, keepdims=True)
    for d in range(1, PEERS):
        send_stat(d, (me + d) % PEERS, me).start()
    landed[me] = part[me]

    for i in range(tiles):
        own_piece(i, me).wait_send()
    for d in range(1, PEERS):
        send_tgt(d, me).wait_send()

    @pl.when(chip < CHIPS - 1)
    def _():
        hop(me, right, send_r).wait_send()

    @pl.when(chip > 0)
    def _():
        hop(me, left, send_l).wait_send()

    for k in range(1, CHIPS):
        @pl.when(chip >= k)
        def _(k=k):
            b = (me + PEERS - CORES * k) % PEERS
            hop(b, other, send_p).wait_send()

            @pl.when(chip < CHIPS - 1)
            def _():
                hop(b, right, send_r).wait_send()

        @pl.when(chip + k < CHIPS)
        def _(k=k):
            b = (me + CORES * k) % PEERS
            hop(b, other, send_p).wait_send()

            @pl.when(chip > 0)
            def _():
                hop(b, left, send_l).wait_send()

    for d in range(1, PEERS):
        send_stat(d, (me + d) % PEERS, (me + PEERS - d) % PEERS).wait()
    got = [landed[b] for b in range(PEERS)]
    m = _tree(jnp.maximum, [g[0:1] for g in got])
    keep = [jnp.exp(g[0:1] - m) for g in got]
    s = _tree(jnp.add, [g[1:2] * k for g, k in zip(got, keep)])
    w = _tree(jnp.add, [g[2:3] * k for g, k in zip(got, keep)])
    lse = m + jnp.log(s)
    logp_ref[...] = _tree(jnp.add, [g[3:4] for g in got]) - lse
    ent_ref[...] = lse - w / s


def solution(mesh):
    def device_body(h, targets, gain, head, tau):
        tok, depth = h.shape[1:]
        vocab = head.shape[0]
        width = CORES * tok
        anywhere = pl.BlockSpec(memory_space=pl.ANY)
        vmem = pl.BlockSpec(memory_space=pltpu.VMEM)
        dma = pltpu.SemaphoreType.DMA
        stat = pltpu.VMEM((8, (CHIPS + 1) * width), F32)
        return pl.pallas_call(
            functools.partial(_kernel, tok, vocab, depth),
            out_shape=[jax.ShapeDtypeStruct((1, tok), F32)] * 2,
            in_specs=[pl.BlockSpec(memory_space=pltpu.SMEM), anywhere, anywhere, vmem, anywhere],
            out_specs=[vmem, vmem],
            scratch_shapes=[
                pltpu.VMEM((PEERS * tok // LANES, depth, LANES), jnp.bfloat16),
                pltpu.VMEM((2, sum(SPLITS), depth), jnp.bfloat16),
                *[pltpu.VMEM((r, width), F32) for r in SPLITS],
                pltpu.VMEM((1, (CHIPS + 1) * width), jnp.int32),
                stat, stat, stat, stat,
                pltpu.VMEM((PEERS, 4, tok), F32),
                pltpu.VMEM((PEERS, 4, tok), F32),
                dma((tok // LANES,)), dma, dma((2,)), dma((tok // LANES,)), dma((tok // LANES,)),
                dma((PEERS,)), dma((PEERS,)), dma((PEERS,)), dma((PEERS,)),
                dma((PEERS,)), dma((PEERS,)), dma((PEERS,)), dma((PEERS,)),
            ],
            compiler_params=pltpu.CompilerParams(
                collective_id=0, has_side_effects=True, vmem_limit_bytes=67_043_328),
        )(tau.reshape(1), h.reshape(tok, depth), targets, gain.reshape(1, depth), head)

    return jax.shard_map(
        device_body,
        mesh=mesh,
        in_specs=(P('dp', 'tp', None), P('dp', 'tp'), P(), P('tp', None), P()),
        out_specs=(P('dp', 'tp'), P('dp', 'tp')),
        check_vma=False,
    )
```

time: 662 us -> 336 us (0.51)
  Pallas kernels: 0 us -> 330 us
  matrix products: 321 us -> 0 us
  waiting for transfers between devices: 187 us -> 0 us
  other arithmetic: 82.8 us -> 0 us
  blocking collectives: 42.3 us -> 0 us
  between operations: 14.7 us -> 1.29 us
  local copies, waits for them, and re-layouts: 14.5 us -> 3.75 us
    pallas_call x0 -> x1, Pallas kernels: none -> 330 us  [device_body(): pl.pallas_call(functools.partial(_kernel, tok, vocab, depth), out_shape=[...]
    dot_general x1 -> x0, matrix products: 321 us -> none  [device_body(): jnp.einsum('rsd,vd->rsv', normed_all, w_loc, preferred_element_type=jnp.f...]
    all_gather x1 -> x0, waiting for transfers between devices: 154 us -> none  [device_body(): normed_all = lax.all_gather(normed, 'tp', axis=1, tiled=True)]
    reduce_sum x2 -> x0, other arithmetic: 77 us -> none  [the longest x1 74.8 us: device_body(): sum_exp = jnp.sum(exp_shift, axis=-1)]
    unnamed x3 -> x0, waiting for transfers between devices: 32.6 us -> none
    pmax x1 -> x0, blocking collectives: 26.7 us -> none  [device_body(): top_val = lax.pmax(local_max, 'tp')]
    all_gather x1 -> x0, blocking collectives: 15.6 us -> none  [device_body(): target_all = lax.all_gather(target_loc, 'tp', axis=1, tiled=True)]
    unnamed x10 -> x2, local copies, waits for them, and re-layouts: 14.1 us -> 2.45 us
  transfers between devices with their start and end apart: 2 -> 0, of which waited for: 2 -> 0; matrix products, arithmetic and copies ran while one was open for 0% -> 0% of each run, Pallas kernels for 0% -> 0%
where the time goes in v1:
time: 336 us
  Pallas kernels  330 us (98%)
  local copies, waits for them, and re-layouts  3.75 us (1%)
    pallas_call x1, Pallas kernels, device_body(): pl.pallas_call(functools.partial(_kernel, tok, vocab, depth), out_shape=[...  330 us

profile of v1, /device:TPU:0, one launch (start us, length us, event | category | flops | bytes accessed | tf_op | source)
XLA Modules:
  0.0 335.5 jit_solution(1205869387777343463)
XLA Ops:
  1.3 1.3 reshape.15.gain_ref
  2.6 330.5 %shard_map.68 = (f32[1,384]{1,0:T(1,128)}, f32[1,384]{1,0:T(1,128)}) custom-call(f32[1]{0:T(128)} %bitcast.2.tau_ref, bf16[384,3072]{1,0:T(8,128)(2,1)} %bitcast.3, s32[1,384]{1,0:T(1,128)} %tgt_hbm.1, bf16[1,3072]{1,0:T(2,128)(2,1)} %reshape.15.gain_ref, bf16[16032,3072]{1,0:T(8,128)(2,1)} %w_hbm.1), custom_call_target="tpu_custom_call" | custom-call | tf_op jit(solution)/shard_map/pallas_call | solution.py:293
  333.1 1.2 copy.10
  334.3 1.2 copy.11

commit v2 on v1

--- a/solution.py
+++ b/solution.py
@@ -15,7 +15,6 @@
 CHIPS = 4
 CORES = 2
 PEERS = CHIPS * CORES
-FORWARD_TRIPS = (5, 10, 15)
 MESH = pl.DeviceIdType.MESH
 
 
@@ -49,7 +48,7 @@
     m_ref[:, cols], s_ref[:, cols], w_ref[:, cols], t_ref[:, cols] = m, s, w, t
 
 
-def _kernel(tok, vocab, depth, tau_ref, h_hbm, tgt_hbm, gain_ref, w_hbm, logp_ref, ent_ref,
+def _kernel(tok, vocab, depth, tau_ref, h_hbm, tgt_hbm, gain_ref, w_hbm, out_ref,
             xs, wbuf, z0, z1, z2, z3, tgt_all, m_ref, s_ref, w_ref, t_ref, part, landed,
             h_sem, t_sem, w_sem, own_send, own_recv, recv, send_p, send_r, send_l, tgt_send, tgt_recv, st_send, st_recv):
     zs = (z0, z1, z2, z3)
@@ -129,7 +128,7 @@
         inv_rms = lax.rsqrt(jnp.sum(acc, axis=-1, keepdims=True) / depth + NORM_EPS)
         for k in range(depth // LANES):
             c = slice(k * LANES, (k + 1) * LANES)
-            v = gain_ref[:, c].astype(F32) * wbuf[1, r, c].astype(F32) * inv_rms
+            v = gain_ref[c].astype(F32).reshape(1, LANES) * wbuf[1, r, c].astype(F32) * inv_rms
             xs[me * tiles + i, c, :] = v.astype(jnp.bfloat16).T
 
     normalise(0)
@@ -199,14 +198,15 @@
         before = jnp.maximum(t - 1, 0)
         at = _xor(chip, p)
         at_before = jnp.where(t == 0, CHIPS, _xor(chip, before // chunks))
-        for k in range(1, CHIPS):
-            @pl.when(t == FORWARD_TRIPS[k - 1])
-            def _(k=k):
-                pass_on(k)
-
-            @pl.when(t == k * chunks)
-            def _(k=k):
-                take_partners(k)
+
+        @pl.when((c == 0) & (p > 0))
+        def _():
+            take_partners(p)
+
+        @pl.when((c == chunks - 1) & (p < CHIPS - 1))
+        def _():
+            pass_on(p + 1)
+
         load_w(t, slot).wait()
 
         @pl.when(t + 1 < trips)
@@ -277,8 +277,8 @@
     s = _tree(jnp.add, [g[1:2] * k for g, k in zip(got, keep)])
     w = _tree(jnp.add, [g[2:3] * k for g, k in zip(got, keep)])
     lse = m + jnp.log(s)
-    logp_ref[...] = _tree(jnp.add, [g[3:4] for g in got]) - lse
-    ent_ref[...] = lse - w / s
+    out_ref[0:1, :] = _tree(jnp.add, [g[3:4] for g in got]) - lse
+    out_ref[1:2, :] = lse - w / s
 
 
 def solution(mesh):
@@ -290,11 +290,11 @@
         vmem = pl.BlockSpec(memory_space=pltpu.VMEM)
         dma = pltpu.SemaphoreType.DMA
         stat = pltpu.VMEM((8, (CHIPS + 1) * width), F32)
-        return pl.pallas_call(
+        out = pl.pallas_call(
             functools.partial(_kernel, tok, vocab, depth),
-            out_shape=[jax.ShapeDtypeStruct((1, tok), F32)] * 2,
+            out_shape=jax.ShapeDtypeStruct((2, tok), F32),
             in_specs=[pl.BlockSpec(memory_space=pltpu.SMEM), anywhere, anywhere, vmem, anywhere],
-            out_specs=[vmem, vmem],
+            out_specs=vmem,
             scratch_shapes=[
                 pltpu.VMEM((PEERS * tok // LANES, depth, LANES), jnp.bfloat16),
                 pltpu.VMEM((2, sum(SPLITS), depth), jnp.bfloat16),
@@ -309,7 +309,8 @@
             ],
             compiler_params=pltpu.CompilerParams(
                 collective_id=0, has_side_effects=True, vmem_limit_bytes=67_043_328),
-        )(tau.reshape(1), h.reshape(tok, depth), targets, gain.reshape(1, depth), head)
+        )(tau.reshape(1), h.reshape(tok, depth), targets, gain, head)
+        return out[0:1], out[1:2]
 
     return jax.shard_map(
         device_body,

time: 336 us -> 331 us (0.985)
  no operation moved by 1% of the time
where the time goes in v2:
time: 331 us
  Pallas kernels  328 us (99%)
    pallas_call x1, Pallas kernels, device_body(): pl.pallas_call(functools.partial(_kernel, tok, vocab, depth), out_shape=j...  328 us

profile of v2, /device:TPU:0, one launch (start us, length us, event | category | flops | bytes accessed | tf_op | source)
XLA Modules:
  0.0 331.1 jit_solution(5968076504882661743)
XLA Ops:
  1.3 328.5 %shard_map.68 = f32[2,384]{1,0:T(2,128)} custom-call(f32[1]{0:T(128)} %bitcast.2.tau_ref, bf16[384,3072]{1,0:T(8,128)(2,1)} %bitcast.3, s32[1,384]{1,0:T(1,128)} %tgt_hbm.1, bf16[3072]{0:T(1024)(128)(2,1)} %gain_ref.1, bf16[16032,3072]{1,0:T(8,128)(2,1)} %w_hbm.1), custom_call_target="tpu_custom_call" | custom-call | tf_op jit(solution)/shard_map/pallas_call | solution.py:293
  329.8 1.3 fusion
